TPU v7x, 128 devices: a whole 4x4x4 slice. The times are simulated.
128 devices in a mesh: col: 16 (over z, x), row: 8 (over y, core).
Axes of the slice: x: 4, y: 4, z: 4, core: 2. Of those that a mesh axis runs over, the one named last changes fastest.
Arguments:
- parent_front: float32 [12288, 12288], P('row', 'col'), as said below
- child_blocks: float32 [8192, 16384], P('row', 'col'), as said below
- child_map: int32 [2, 64], replicated, may hold values from 0 to 95, as said below
- child_order: int32 [2], replicated, may hold values from 4096 to 8192, as said below
Outputs:
- factored: float32 [12288, 12288], P('row', 'col')
Inputs may be any that keep to these rules, and one draw needn't show every extreme that they name: parent_front is symmetric. `child_blocks`: each child's block, in true tile order, is symmetric. `child_map`: along each child's 64 tiles the parent tile numbers rise strictly. `child_order`: one child has exactly 8192; every child has at least 4096.
All inputs are finite; a program needn't handle non-finite values.
Results may differ from a plain program's by a relative error of at most 0.0001.
Values sent between devices are 32-bit elements; how exact they have to be, the bound alone decides.
A program may use at most 128 MiB of HBM per device.

v0:
```python
import jax
import jax.numpy as jnp
from jax import lax
from jax.sharding import PartitionSpec as P

B = 128
NPIV = 256


HIGHEST_PRECISION = lax.Precision.HIGHEST


def broadcast(value, axis, source):
    kept = jnp.where(lax.axis_index(axis) == source, value, 0).astype(value.dtype)
    return lax.psum(kept, axis)


def plan_slots(targets, usable, block_size, dest_count, slot_count):
    item_total = targets.shape[0]
    places = jnp.arange(item_total, dtype=jnp.int32)
    owners = targets // block_size
    within = targets % block_size
    earlier = (
        (owners[:, None] == owners[None, :]) & usable[None, :] & (places[None, :] < places[:, None])
    )
    ranking = jnp.sum(earlier.astype(jnp.int32), axis=1)
    picked = (
        usable[None, None, :]
        & (owners[None, None, :] == jnp.arange(dest_count, dtype=jnp.int32)[:, None, None])
        & (ranking[None, None, :] == jnp.arange(slot_count, dtype=jnp.int32)[None, :, None])
    )
    filled = jnp.any(picked, axis=2)
    source = jnp.sum(jnp.where(picked, places[None, None, :], 0), axis=2)
    labels = jnp.where(filled, jnp.sum(jnp.where(picked, within[None, None, :], 0), axis=2), -1)
    return (source, filled, labels)


def child_targets(child_map, child_order, child_index, tile_numbers):
    chosen = jnp.arange(child_map.shape[0], dtype=jnp.int32) == child_index
    row_map = jnp.sum(jnp.where(chosen[:, None], child_map, 0), axis=0)
    order_limit = jnp.sum(jnp.where(chosen, child_order, 0))
    onehot = tile_numbers[:, None] == jnp.arange(row_map.shape[0], dtype=jnp.int32)[None, :]
    targets = jnp.sum(jnp.where(onehot, row_map[None, :], 0), axis=1)
    return (targets, tile_numbers * B < order_limit)


def shards(parent_front, child_blocks, child_map, child_order):
    rows_grid = lax.axis_size("row")
    cols_grid = lax.axis_size("col")
    row_index = lax.axis_index("row")
    col_index = lax.axis_index("col")
    local_rows, local_cols = parent_front.shape
    kid_rows, kid_cols = child_blocks.shape
    kid_count = child_map.shape[0]
    per_child = cols_grid // kid_count
    my_child = col_index // per_child
    my_slot = col_index % per_child
    tiles_down = kid_rows // B
    tiles_across = kid_cols // B
    parent_rtiles = local_rows // B
    parent_ctiles = local_cols // B
    cap_rows = (parent_rtiles + rows_grid - 1) // rows_grid
    cap_cols = (parent_ctiles + per_child - 1) // per_child
    row_tiles = jnp.arange(tiles_down, dtype=jnp.int32) * rows_grid + row_index
    col_tiles = jnp.arange(tiles_across, dtype=jnp.int32) * per_child + my_slot
    chosen = jnp.arange(kid_count, dtype=jnp.int32) == my_child
    order_limit = jnp.sum(jnp.where(chosen, child_order, 0))
    within = jnp.arange(B, dtype=jnp.int32)
    row_alive = (row_tiles[:, None] * B + within[None, :]).reshape(-1) < order_limit
    col_alive = (col_tiles[:, None] * B + within[None, :]).reshape(-1) < order_limit
    children = jnp.where(row_alive[:, None] & col_alive[None, :], child_blocks, 0.0)
    col_targets, col_usable = child_targets(child_map, child_order, my_child, col_tiles)
    row_targets, row_usable = child_targets(child_map, child_order, my_child, row_tiles)
    source, filled, labels = plan_slots(row_targets, row_usable, parent_rtiles, rows_grid, cap_rows)
    row_tiled = children.reshape(tiles_down, B, kid_cols)
    outgoing = jnp.where(filled[:, :, None, None], row_tiled[source], 0.0)
    arrived, arrived_labels = (
        lax.all_to_all(outgoing, "row", split_axis=0, concat_axis=0, tiled=True),
        lax.all_to_all(labels, "row", split_axis=0, concat_axis=0, tiled=True),
    )
    flat_labels = arrived_labels.reshape(-1)
    flat_tiles = arrived.reshape(-1, B, kid_cols)
    slots_here = flat_labels.shape[0]
    matches = flat_labels[None, :] == jnp.arange(parent_rtiles, dtype=jnp.int32)[:, None]
    present = jnp.any(matches, axis=1)
    pick_slot = jnp.sum(
        jnp.where(matches, jnp.arange(slots_here, dtype=jnp.int32)[None, :], 0), axis=1
    )
    framed = jnp.where(present[:, None, None], flat_tiles[pick_slot], 0.0).reshape(
        local_rows, kid_cols
    )
    col_source, col_filled, col_labels = plan_slots(
        col_targets, col_usable, parent_ctiles, cols_grid, cap_cols
    )
    columns = framed.reshape(local_rows, tiles_across, B)
    outgoing_cols = jnp.where(col_filled[None, :, :, None], columns[:, col_source], 0.0)
    arrived_cols, labels_back = (
        lax.all_to_all(outgoing_cols, "col", split_axis=1, concat_axis=1, tiled=True),
        lax.all_to_all(col_labels[None], "col", split_axis=1, concat_axis=1, tiled=True),
    )
    landing = (
        labels_back.reshape(-1)[:, None] == jnp.arange(parent_ctiles, dtype=jnp.int32)[None, :]
    ).astype(jnp.float32)
    assembled = jnp.einsum(
        "rsb,su->rub",
        arrived_cols.reshape(local_rows, -1, B),
        landing,
        precision=HIGHEST_PRECISION,
        preferred_element_type=jnp.float32,
    ).reshape(local_rows, local_cols)
    front_local = parent_front + assembled
    panel_width = B
    step_count = NPIV // panel_width
    global_rows = row_index * local_rows + jnp.arange(local_rows, dtype=jnp.int32)
    global_cols = col_index * local_cols + jnp.arange(local_cols, dtype=jnp.int32)
    zero_index = jnp.int32(0)

    def fetch_panel(piece_cols, panel_start):
        return broadcast(piece_cols, "col", panel_start // local_cols)

    def finish(raw_panel, panel_start):
        holder = panel_start // local_rows
        offset = panel_start % local_rows
        corner = lax.dynamic_slice(raw_panel, (offset, zero_index), (panel_width, panel_width))
        corner = broadcast(corner, "row", holder)
        factor = jnp.linalg.cholesky(corner)
        solved = lax.linalg.triangular_solve(
            factor, raw_panel, left_side=False, lower=True, transpose_a=True
        )
        placed = lax.dynamic_update_slice(
            solved, factor, (panel_start - row_index * local_rows, zero_index)
        )
        in_corner = (global_rows >= panel_start) & (global_rows < panel_start + panel_width)
        left_rows = jnp.where(
            global_rows[:, None] < panel_start, 0.0, jnp.where(in_corner[:, None], placed, solved)
        )
        col_base = col_index * local_cols
        sender = col_base // local_rows
        part_rows = lax.dynamic_slice(
            left_rows, (col_base % local_rows, zero_index), (local_cols, panel_width)
        )
        across = broadcast(part_rows, "row", sender)
        return (left_rows, across)

    def apply_update(front_now, left_rows, across, panel_start):
        panel_end = panel_start + panel_width
        trailing = (global_rows[:, None] >= panel_end) & (global_cols[None, :] >= panel_end)
        product = lax.dot_general(
            left_rows,
            across,
            (((1,), (1,)), ((), ())),
            precision=HIGHEST_PRECISION,
            preferred_element_type=jnp.float32,
        )
        front_now = jnp.where(trailing, front_now - product, front_now)
        written = lax.dynamic_update_slice(
            front_now, left_rows, (zero_index, panel_start % local_cols)
        )
        in_panel = (global_cols >= panel_start) & (global_cols < panel_end)
        return jnp.where(in_panel[None, :], written, front_now)

    def advance_plain(step_number, front_now):
        panel_start = step_number * panel_width
        raw_panel = fetch_panel(
            lax.dynamic_slice(
                front_now, (zero_index, panel_start % local_cols), (local_rows, panel_width)
            ),
            panel_start,
        )
        left_rows, across = finish(raw_panel, panel_start)
        return apply_update(front_now, left_rows, across, panel_start)

    front_local = lax.fori_loop(0, step_count, advance_plain, front_local)
    upper_part = (global_rows[:, None] < NPIV) & (global_cols[None, :] >= NPIV)
    return jnp.where(upper_part, 0.0, front_local)


def solution(mesh):
    placed = (P("row", "col"), P("row", "col"), P(), P())
    return jax.shard_map(
        shards, mesh=mesh, in_specs=placed, out_specs=P("row", "col"), check_vma=False
    )
```

profile of v0, /device:TPU:39, one launch (start us, length us, event | category | flops | bytes accessed | tf_op | source)
XLA Modules:
  0.0 919.8 jit_solution(13344825785148846199)
XLA Ops:
  6.5 1.3 select_reduce_fusion.7
  7.8 0.8 select_reduce_fusion.6
  8.8 0.7 broadcast_compare_fusion.1
  10.0 0.7 copy.50
  10.7 5.1 all-to-all-start.1
  15.9 0.7 fusion.31
  16.7 0.7 fusion.30
  17.6 4.7 and_select_fusion.1
  22.2 6.5 gather_fusion
  28.7 8.6 broadcast_select_fusion.1
  37.3 4.9 all-to-all-start.2
  42.7 0.7 copy.49
  43.4 0.5 broadcast.871
  43.9 0.6 reduce.29
  44.9 91.3 %all-to-all-done.2 = f32[8,2,128,1024]{3,2,1,0:T(8,128)} async-done(((f32[8,2,128,1024]{3,2,1,0:T(8,128)}), f32[8,2,128,1024]{3,2,1,0:T(8,128)}, u32[]{:S(2)}, u32[]{:S(2)}) %all-to-all-start.2) | async-done | bytes 8388640 | tf_op jit(solution)/shard_map/all_to_all | solution.py:78
  136.1 7.3 all-to-all-start
  143.4 7.0 gather_fusion.1
  150.4 4.3 copy.59
  154.7 3.5 copy_select_fusion
  158.2 8.6 gather_fusion.2
  166.8 10.4 %fusion.13 = f32[1536,16,1,128]{3,0,2,1:T(8,128)} fusion(f32[16,1536,128]{2,1,0:T(8,128)} %gather_fusion.2, pred[16]{0:T(512)(128)(4,1)S(1)} %fusion.32), kind=kLoop, calls=%fused_computation.32 | loop fusion | flops 3145728 | bytes 25165840 | tf_op jit(solution)/shard_map/jit(_where)/select_n | solution.py:96
  177.2 6.7 all-to-all-start.3
  183.8 6.0 copy.57
  190.3 173.0 %all-to-all-done.3 = f32[1536,16,1,128]{3,0,2,1:T(8,128)} async-done(((f32[1536,16,1,128]{3,0,2,1:T(8,128)}), f32[1536,16,1,128]{3,0,2,1:T(8,128)}, u32[]{:S(2)}, u32[]{:S(2)}) %all-to-all-start.3) | async-done | bytes 12582944 | tf_op jit(solution)/shard_map/all_to_all | solution.py:98
  363.3 19.7 %fusion.17 = f32[1536,6,128]{2,1,0:T(8,128)} fusion(f32[1536,16,1,128]{3,0,2,1:T(8,128)} %all-to-all-done.3, s32[16]{0:T(128)S(1)} %reduce.25), kind=kOutput, calls=%fused_computation.41 | convolution fusion | flops 226492512 | bytes 17301568 | tf_op jit(solution)/shard_map/rsb,su->rub/dot_general | solution.py:104
  382.9 6.0 copy.56
  389.0 6.9 bitcast_add_fusion.1
  395.9 6.0 copy.58
  402.0 505.9 %while.18 = (s32[]{:T(128)}, f32[1536,768]{1,0:T(8,128)}, s32[]{:T(128)}, s32[]{:T(128)}, s32[]{:T(128)}, /*index=5*/s32[]{:T(128)}, s32[]{:T(128)}, s32[]{:T(12...) while((s32[]{:T(128)}, f32[1536,768]{1,0:T(8,128)}, ...), condition=%wide.region_20.21_spmd.clone.clone, body=%wide.region_14.20_spmd.clone.clone.sunk | while | flops 2118905600 | bytes 28462080 | solution.py:173
  402.0 2.6 dynamic-slice_select_fusion.8
  404.7 87.5 %all-reduce.4.cloned.1.call-done = f32[1536,128]{1,0:T(8,128)} async-done(((f32[1536,128]{1,0:T(8,128)}), f32[1536,128]{1,0:T(8,128)}) %all-reduce.4.cloned.1.call-update) | async-done | bytes 786448 | tf_op jit(solution)/shard_map/while/body/eval_jaxpr/psum | solution.py:15
  492.2 1.5 dynamic-slice_select_fusion.9
  493.8 60.4 %all-reduce.6.cloned.1.call-done = f32[128,128]{1,0:T(8,128)} async-done(((f32[128,128]{1,0:T(8,128)}), f32[128,128]{1,0:T(8,128)}) %all-reduce.6.cloned.1.call-update) | async-done | bytes 65552 | tf_op jit(solution)/shard_map/while/body/eval_jaxpr/psum | solution.py:15
  554.2 0.9 copy.68
  555.2 0.9 fusion.54
  556.0 11.7 %cholesky.80 = f32[128,128]{1,0:T(8,128)S(1)} custom-call(f32[128,128]{1,0:T(8,128)S(1)} %fusion.54), custom_call_target="Cholesky" | custom-call | tf_op jit(solution)/shard_map/while/body/eval_jaxpr/jit(cholesky)/cholesky | solution.py:126
  567.8 0.6 compare_reduce_fusion.2
  568.4 0.7 select_bitcast_fusion.4
  569.1 9.8 %custom-call.31 = f32[1,128,128]{1,2,0:T(8,128)S(1)} custom-call(f32[1,128,128]{2,1,0:T(8,128)S(1)} %select_bitcast_fusion.4), custom_call_target="InvertDiagBlocksLowerTriangular" | custom-call | tf_op jit(solution)/shard_map/while/body/eval_jaxpr/triangular_solve | solution.py:127
  578.9 1.9 fusion.55
  580.8 0.7 select_dynamic-update-slice_fusion.2
  581.8 0.8 dynamic-slice_select_fusion.10
  582.8 59.5 %all-reduce.8.cloned.1.call-done = f32[768,128]{1,0:T(8,128)} async-done(((f32[768,128]{1,0:T(8,128)}), f32[768,128]{1,0:T(8,128)}) %all-reduce.8.cloned.1.call-update) | async-done | bytes 393232 | tf_op jit(solution)/shard_map/while/body/eval_jaxpr/psum | solution.py:15
  642.2 7.5 subtract_select_fusion.2
  649.7 1.9 dynamic-slice_select_fusion.11
  651.6 4.8 select_n.633
  656.4 2.6 dynamic-slice_select_fusion.8
  659.1 84.7 %all-reduce.4.cloned.1.call-done = f32[1536,128]{1,0:T(8,128)} async-done(((f32[1536,128]{1,0:T(8,128)}), f32[1536,128]{1,0:T(8,128)}) %all-reduce.4.cloned.1.call-update) | async-done | bytes 786448 | tf_op jit(solution)/shard_map/while/body/eval_jaxpr/psum | solution.py:15
  743.8 1.5 dynamic-slice_select_fusion.9
  745.5 60.2 %all-reduce.6.cloned.1.call-done = f32[128,128]{1,0:T(8,128)} async-done(((f32[128,128]{1,0:T(8,128)}), f32[128,128]{1,0:T(8,128)}) %all-reduce.6.cloned.1.call-update) | async-done | bytes 65552 | tf_op jit(solution)/shard_map/while/body/eval_jaxpr/psum | solution.py:15
  805.8 0.9 copy.68
  806.7 0.9 fusion.54
  807.6 11.7 %cholesky.80 = f32[128,128]{1,0:T(8,128)S(1)} custom-call(f32[128,128]{1,0:T(8,128)S(1)} %fusion.54), custom_call_target="Cholesky" | custom-call | tf_op jit(solution)/shard_map/while/body/eval_jaxpr/jit(cholesky)/cholesky | solution.py:126
  819.3 0.6 compare_reduce_fusion.2
  819.9 0.7 select_bitcast_fusion.4
  820.6 9.8 %custom-call.31 = f32[1,128,128]{1,2,0:T(8,128)S(1)} custom-call(f32[1,128,128]{2,1,0:T(8,128)S(1)} %select_bitcast_fusion.4), custom_call_target="InvertDiagBlocksLowerTriangular" | custom-call | tf_op jit(solution)/shard_map/while/body/eval_jaxpr/triangular_solve | solution.py:127
  830.4 1.9 fusion.55
  832.3 0.7 select_dynamic-update-slice_fusion.2
  833.3 0.8 dynamic-slice_select_fusion.10
  834.3 59.5 %all-reduce.8.cloned.1.call-done = f32[768,128]{1,0:T(8,128)} async-done(((f32[768,128]{1,0:T(8,128)}), f32[768,128]{1,0:T(8,128)}) %all-reduce.8.cloned.1.call-update) | async-done | bytes 393232 | tf_op jit(solution)/shard_map/while/body/eval_jaxpr/psum | solution.py:15
  893.7 7.5 subtract_select_fusion.2
  901.3 1.9 dynamic-slice_select_fusion.11
  903.1 4.7 select_n.633
  907.9 5.1 and_select_fusion
  (63 shorter events, 3.5 us)
Async XLA Ops:
  10.7 26.6 %all-to-all-start.1 = ((s32[8,1,2]{2,1,0:T(1,128)}), s32[8,1,2]{2,1,0:T(1,128)S(1)}, u32[]{:S(2)}, u32[]{:S(2)}) async-start(s32[8,1,2]{2,1,0:T(1,128)} %copy.50), calls=%async_computation.1 | async-start | bytes 8192 | tf_op jit(solution)/shard_map/all_to_all | solution.py:79
  37.3 98.8 %all-to-all-start.2 = ((f32[8,2,128,1024]{3,2,1,0:T(8,128)}), f32[8,2,128,1024]{3,2,1,0:T(8,128)}, u32[]{:S(2)}, u32[]{:S(2)}) async-start(f32[8,2,128,1024]{3,2,1,0:T(8,128)} %broadcast_select_fusion.1), calls=%async_computation.2 | async-start | bytes 16777216 | tf_op jit(solution)/shard_map/all_to_all | solution.py:78
  136.1 41.0 %all-to-all-start = ((s32[1,16,1]{2,0,1:T(1,128)}), s32[1,16,1]{2,0,1:T(1,128)S(1)}, u32[]{:S(2)}, u32[]{:S(2)}) async-start(s32[1,16,1]{2,0,1:T(1,128)} %copy.49), calls=%async_computation | async-start | bytes 16384 | tf_op jit(solution)/shard_map/all_to_all | solution.py:99
  177.2 186.1 %all-to-all-start.3 = ((f32[1536,16,1,128]{3,0,2,1:T(8,128)}), f32[1536,16,1,128]{3,0,2,1:T(8,128)}, u32[]{:S(2)}, u32[]{:S(2)}) async-start(f32[1536,16,1,128]{3,0,2,1:T(8,128)} %fusion.13), calls=%async_computation.3 | async-start | bytes 25165824 | tf_op jit(solution)/shard_map/all_to_all | solution.py:98
  402.0 90.2 %all-reduce.4.cloned.1.call-start = ((), (), s32[]{:S(2)}) async-start(), calls=%async_computation.4 | async-start | bytes 1572864 | tf_op jit(solution)/shard_map/while/body/eval_jaxpr/psum | solution.py:15
  404.5 149.7 %all-reduce.6.cloned.1.call-start = ((), (), s32[]{:S(2)}) async-start(), calls=%async_computation.5 | async-start | bytes 131072 | tf_op jit(solution)/shard_map/while/body/eval_jaxpr/psum | solution.py:15
  493.7 148.5 %all-reduce.8.cloned.1.call-start = ((), (), s32[]{:S(2)}) async-start(), calls=%async_computation.6 | async-start | bytes 786432 | tf_op jit(solution)/shard_map/while/body/eval_jaxpr/psum | solution.py:15
  656.4 87.4 %all-reduce.4.cloned.1.call-start = ((), (), s32[]{:S(2)}) async-start(), calls=%async_computation.4 | async-start | bytes 1572864 | tf_op jit(solution)/shard_map/while/body/eval_jaxpr/psum | solution.py:15
  659.0 146.8 %all-reduce.6.cloned.1.call-start = ((), (), s32[]{:S(2)}) async-start(), calls=%async_computation.5 | async-start | bytes 131072 | tf_op jit(solution)/shard_map/while/body/eval_jaxpr/psum | solution.py:15
  745.4 148.3 %all-reduce.8.cloned.1.call-start = ((), (), s32[]{:S(2)}) async-start(), calls=%async_computation.6 | async-start | bytes 786432 | tf_op jit(solution)/shard_map/while/body/eval_jaxpr/psum | solution.py:15
Sparse Core Ops, SparseCore 0:
  406.0 86.0 all-reduce.3
  494.6 59.6 all-reduce.5
  582.8 59.3 all-reduce.7
  660.2 83.6 all-reduce.3
  746.1 59.6 all-reduce.5
  834.3 59.3 all-reduce.7
where the time goes:
time: 924 us; the launch traced here: 920 us
  waiting for transfers between devices  676 us (73%)
  other arithmetic  109 us (12%)
  local copies, waits for them, and re-layouts  58.3 us (6%)
  matrix products  38.6 us (4%)
  starting transfers between devices  24.2 us (3%)
  between operations  13.5 us (1%)
    psum x6, waiting for transfers between devices, broadcast(): return lax.psum(kept, axis)  412 us
    all_to_all x1, waiting for transfers between devices, shards(): lax.all_to_all(outgoing_cols, 'col', split_axis=1, concat_axis=1, tiled=T...  173 us
    all_to_all x1, waiting for transfers between devices, shards(): lax.all_to_all(outgoing, 'row', split_axis=0, concat_axis=0, tiled=True)  91.3 us
    another operation x6, other arithmetic, finish(): factor = jnp.linalg.cholesky(corner)  24.8 us
    another operation x4, other arithmetic, finish(): lax.linalg.triangular_solve(factor, raw_panel, left_side=False, lower=Tru...  20.9 us
    dot_general x1, matrix products, shards(): jnp.einsum('rsb,su->rub', arrived_cols.reshape(local_rows, -1, B), landin...  19.7 us
  transfers between devices with their start and end apart: 10, of which 8 were waited for; matrix products, arithmetic and copies ran while one was open for 7% of the time, Pallas kernels for 0%

commit v1 on v0

v1 whole, which is shorter than its diff:
```python
import functools

import jax
import jax.numpy as jnp
from jax import lax
from jax.experimental import pallas as pl
from jax.experimental.pallas import tpu as pltpu
from jax.sharding import PartitionSpec as P

B = 128
NPIV = 256
ROWS = 8
COLS = 16
PARTS = 4
SUB = B // PARTS
MESH = pl.DeviceIdType.MESH
HI = lax.Precision.HIGHEST
VMEM_LIMIT = 66 * 1000 * 1000

T_INV = 0
T_SEL = 192
T_COL = 384
T_ROW = 640
T_ORD = 832
T_LEN = 834


def routing_table(child_map, child_order):
    kids, tiles = child_map.shape
    tile = jnp.arange(tiles, dtype=jnp.int32)
    place = jnp.arange(96, dtype=jnp.int32)
    hit = child_map[:, None, :] == place[None, :, None]
    inverse = jnp.sum(jnp.where(hit, tile[None, None, :] + 1, 0), axis=2) - 1
    window = child_map // 12
    same = (
        ((tile[:, None] - tile[None, :]) % ROWS == 0)
        & (tile[None, :] < tile[:, None])
    )
    rank = jnp.sum(
        (same[None] & (window[:, :, None] == window[:, None, :])).astype(jnp.int32), axis=2
    )
    slot = tile[None, :] % ROWS + ROWS * rank
    select = jnp.sum(jnp.where(hit, slot[:, None, :], 0), axis=2)
    grouped = child_map.reshape(kids, 8, 8)
    dest = jnp.arange(COLS, dtype=jnp.int32)
    step = jnp.arange(8, dtype=jnp.int32)
    col_pick = jnp.sum(
        jnp.where(
            (grouped // 6)[:, :, :, None] == dest[None, None, None, :],
            step[None, :, None, None],
            0,
        ),
        axis=1,
    )
    edges = jnp.arange(9, dtype=jnp.int32) * 12
    count = jnp.sum((grouped[:, :, :, None] < edges).astype(jnp.int32), axis=1)
    low, mid = count[:, :, 0:8:2], count[:, :, 1:9:2]
    extra = jnp.where(mid - low == 2, low + 1, mid + 1)
    row_pick = jnp.minimum(jnp.stack([low, mid, extra], axis=-1), 7)
    return jnp.concatenate(
        [
            inverse.reshape(-1),
            select.reshape(-1),
            col_pick.reshape(-1),
            row_pick.reshape(-1),
            child_order.reshape(-1),
        ]
    ).astype(jnp.int32)


def enter(row, col):
    barrier = pltpu.get_barrier_semaphore()
    for d in range(1, COLS):
        pl.semaphore_signal(
            barrier,
            inc=1,
            device_id={"col": lax.rem(col + d, COLS)},
            device_id_type=MESH,
        )
    for d in range(1, ROWS):
        pl.semaphore_signal(
            barrier,
            inc=1,
            device_id={"row": lax.rem(row + d, ROWS)},
            device_id_type=MESH,
        )
    pl.semaphore_wait(barrier, COLS + ROWS - 2)


def extend_kernel(tab, parent, child, out, kid_cols, load_sem, send_c, send_r, *rest):
    recv_c = rest[:PARTS]
    recv_r = rest[PARTS : 2 * PARTS]
    cs, cr, rs, dr, br, fs = rest[2 * PARTS :]
    row = lax.axis_index("row")
    col = lax.axis_index("col")
    chip = row // 2
    core = lax.rem(row, 2)
    other = 1 - core
    mate = row + 1 - 2 * core
    kid = col // 8
    slot = lax.rem(col, 8)
    loads = [
        pltpu.make_async_copy(
            child.at[:, k * B : (k + 1) * B], kid_cols.at[k], load_sem.at[k]
        )
        for k in range(8)
    ]
    for load in loads:
        load.start()
    enter(row, col)
    for load in loads:
        load.wait()

    def take_col(g, dest):
        k = tab[T_COL + (kid * 8 + slot) * COLS + dest]
        return [kid_cols[k, t * B + g * SUB : t * B + (g + 1) * SUB, :] for t in range(8)]

    def col_copy(g, d):
        dest = lax.rem(col + d, COLS)
        return pltpu.make_async_remote_copy(
            src_ref=send_c.at[g, dest],
            dst_ref=recv_c[g].at[col],
            send_sem=cs.at[g, d],
            recv_sem=cr.at[g, col],
            device_id={"col": dest},
            device_id_type=MESH,
        )

    def col_arrival(g, d):
        source = lax.rem(col + d, COLS)
        return pltpu.make_async_remote_copy(
            src_ref=send_c.at[g, source],
            dst_ref=recv_c[g].at[source],
            send_sem=cs.at[g, d],
            recv_sem=cr.at[g, source],
            device_id={"col": source},
            device_id_type=MESH,
        )

    for g in range(PARTS):

        @pl.loop(1, COLS)
        def _(d):
            dest = lax.rem(col + d, COLS)
            for t, piece in enumerate(take_col(g, dest)):
                send_c[g, dest, t] = piece

        for t, piece in enumerate(take_col(g, col)):
            recv_c[g][col, t] = piece

        @pl.loop(1, COLS)
        def _(d):
            col_copy(g, d).start()

    def direct_copy(g, dy, side):
        chip_to = lax.rem(chip + dy, 4)
        return pltpu.make_async_remote_copy(
            src_ref=send_r.at[g, chip_to * 3 + side],
            dst_ref=recv_r[g].at[row],
            send_sem=rs.at[g, dy * 3 + side],
            recv_sem=dr.at[g, row],
            device_id={"row": chip_to * 2 + side},
            device_id_type=MESH,
        )

    def mate_copy(g):
        return pltpu.make_async_remote_copy(
            src_ref=send_r.at[g, chip * 3 + other],
            dst_ref=recv_r[g].at[row],
            send_sem=rs.at[g, 0],
            recv_sem=dr.at[g, row],
            device_id={"row": mate},
            device_id_type=MESH,
        )

    def extra_copy(g, dy):
        chip_to = lax.rem(chip + dy, 4)
        return pltpu.make_async_remote_copy(
            src_ref=send_r.at[g, chip_to * 3 + 2],
            dst_ref=recv_r[g].at[8 + row],
            send_sem=rs.at[g, dy * 3 + 2],
            recv_sem=br.at[g, row],
            device_id={"row": chip_to * 2 + core},
            device_id_type=MESH,
        )

    def row_arrival(g, source, base, sem):
        return pltpu.make_async_remote_copy(
            src_ref=send_r.at[g, 0],
            dst_ref=recv_r[g].at[base + source],
            send_sem=rs.at[g, 0],
            recv_sem=sem.at[g, source],
            device_id={"row": source},
            device_id_type=MESH,
        )

    def forward_copy(g, dy):
        source = lax.rem(chip + dy, 4) * 2 + core
        return pltpu.make_async_remote_copy(
            src_ref=recv_r[g].at[8 + source],
            dst_ref=recv_r[g].at[8 + source],
            send_sem=fs.at[g, dy],
            recv_sem=br.at[g, source],
            device_id={"row": mate},
            device_id_type=MESH,
        )

    def spread_rows(g):
        @pl.loop(1, COLS)
        def _(d):
            col_arrival(g, d).wait_recv()

        sources = []
        for h in range(2):
            for b in range(6):
                j = jnp.maximum(tab[T_INV + h * 96 + col * 6 + b], 0)
                sources.append(h * 8 + lax.rem(j, 8))

        @pl.loop(0, 12)
        def _(q):
            for h in range(2):
                k = tab[T_ROW + (h * 8 + row) * 12 + q]
                for b in range(6):
                    send_r[g, q, h, :, b * B : (b + 1) * B] = recv_c[g][sources[h * 6 + b], k]

        recv_r[g][row] = send_r[g, chip * 3 + core]
        recv_r[g][8 + row] = send_r[g, chip * 3 + 2]
        for dy in (2, 1, 3):
            direct_copy(g, dy, 0).start()
            direct_copy(g, dy, 1).start()
            extra_copy(g, dy).start()
        mate_copy(g).start()
        forward_copy(g, 0).start()

    def forward(g):
        for dy in range(1, 4):
            row_arrival(g, lax.rem(chip + dy, 4) * 2 + core, 8, br).wait_recv()
            forward_copy(g, dy).start()

    def land(g):
        for d in range(1, ROWS):
            row_arrival(g, lax.rem(row + d, ROWS), 0, dr).wait_recv()
        for dy in range(4):
            row_arrival(g, lax.rem(chip + dy, 4) * 2 + other, 8, br).wait_recv()
        lane = lax.broadcasted_iota(jnp.int32, (1, B), 1)
        alive = []
        for h in range(2):
            order = tab[T_ORD + h]
            for b in range(6):
                j = tab[T_INV + h * 96 + col * 6 + b]
                limit = jnp.where(j < 0, 0, order - j * B)
                alive.append(lane < limit)
        down = lax.broadcasted_iota(jnp.int32, (SUB, 1), 0) + g * SUB

        @pl.loop(0, 12)
        def _(a):
            start = pl.multiple_of(a * B + g * SUB, SUB)
            picks, lives = [], []
            for h in range(2):
                place = h * 96 + row * 12 + a
                i = tab[T_INV + place]
                limit = jnp.where(i < 0, 0, tab[T_ORD + h] - i * B)
                picks.append(tab[T_SEL + place])
                lives.append(down < limit)
            for b in range(6):
                span = slice(b * B, (b + 1) * B)
                total = parent[pl.ds(start, SUB), span]
                for h in range(2):
                    piece = recv_r[g][picks[h], h, :, span]
                    total = total + jnp.where(lives[h] & alive[h * 6 + b], piece, 0.0)
                out[pl.ds(start, SUB), span] = total

    for g in range(PARTS):
        spread_rows(g)
        if g >= 1:
            forward(g - 1)
        if g >= 2:
            land(g - 2)
    forward(PARTS - 1)
    for g in range(max(PARTS - 2, 0), PARTS):
        land(g)

    for g in range(PARTS):

        @pl.loop(1, COLS)
        def _(d):
            col_copy(g, d).wait_send()

        for dy in range(1, 4):
            direct_copy(g, dy, 0).wait_send()
            direct_copy(g, dy, 1).wait_send()
            extra_copy(g, dy).wait_send()
        mate_copy(g).wait_send()
        for dy in range(4):
            forward_copy(g, dy).wait_send()


def mul(a, b, ca, cb):
    return lax.dot_general(
        a,
        b,
        (((ca,), (cb,)), ((), ())),
        precision=HI,
        preferred_element_type=jnp.float32,
    )


def eliminate(work):
    wide = lax.broadcasted_iota(jnp.int32, (B, B), 1)
    tall = lax.broadcasted_iota(jnp.int32, (B, B), 0)
    one = lax.broadcasted_iota(jnp.int32, (1, B), 1)
    down = lax.broadcasted_iota(jnp.int32, (B, 1), 0)

    def body(j, carry):
        pivot_row = work[pl.ds(j, 1), :]
        pivot = jnp.sum(jnp.where(one == j, pivot_row[:, :B], 0.0), axis=1, keepdims=True)
        column = jnp.sum(jnp.where(wide == j, work[:, :B], 0.0), axis=1, keepdims=True)
        factor = jnp.where(down > j, column / pivot, 0.0)
        work[...] = work[...] - factor * pivot_row
        return carry

    lax.fori_loop(0, B - 1, body, 0)
    upper = work[:, :B]
    diagonal = jnp.sum(jnp.where(wide == tall, upper, 0.0), axis=1, keepdims=True)
    scale = lax.rsqrt(diagonal)
    scale = scale * (1.5 - 0.5 * diagonal * scale * scale)
    upper_factor = jnp.where(wide >= tall, upper * scale, 0.0)
    inverse = jnp.where(wide <= tall, work[:, B:] * scale, 0.0)
    return upper_factor, inverse


def factor_kernel(
    front, out, corner, mine, rows_ref, work, lower, inv, left, right, s_a, r_a, s_u, r_u, s_p, r_p
):
    row = lax.axis_index("row")
    col = lax.axis_index("col")
    chip = row // 2
    core = lax.rem(row, 2)
    zed = col // 4
    ex = lax.rem(col, 4)
    enter(row, col)

    def copy(src, dst, send, recv, **where):
        return pltpu.make_async_remote_copy(
            src_ref=src,
            dst_ref=dst,
            send_sem=send,
            recv_sem=recv,
            device_id=where,
            device_id_type=MESH,
        )

    def corner_copy(index, **where):
        return copy(corner, corner, s_a.at[index], r_a, **where)

    def mine_copy(index, **where):
        return copy(mine, mine, s_u.at[index], r_u, **where)

    piece = lax.rem(ex, 2)

    def z_copy(d):
        to = lax.rem(zed + d, 4) * 4 + ex
        return copy(mine, rows_ref.at[piece], s_p.at[d - 1], r_p.at[piece], col=to)

    def x_copy(d):
        to = zed * 4 + lax.rem(ex + d, 4)
        return copy(
            rows_ref.at[piece], rows_ref.at[piece], s_p.at[2 + d], r_p.at[piece], col=to
        )

    def piece_arrival(index):
        return copy(mine, rows_ref.at[index], s_p.at[0], r_p.at[index], col=col)

    owner = col // 2 == row
    holder = ex // 2 == core
    top = row == 0
    first = top & (col == 0)
    relay = (core == 0) & (row > 0)

    @pl.when(top)
    def _():
        mine[...] = front[0:NPIV, :]

    @pl.when(first)
    def _():
        corner[...] = front[0:NPIV, 0:NPIV]
        for d in (2, 8, 1, 3, 4, 12, 5, 6, 7, 9, 10, 11, 13, 14, 15):
            corner_copy(d, col=d).start()

    @pl.when(jnp.logical_not(first))
    def _():
        corner_copy(0, col=col).wait_recv()

    @pl.when(top)
    def _():
        for d in (4, 2, 6, 1):
            corner_copy(15 + d, row=d).start()
        for d in (4, 2, 6, 1):
            mine_copy(d, row=d).start()

    @pl.when(relay)
    def _():
        corner_copy(16, row=row + 1).start()

    work[:, :B] = corner[:B, :B]
    tall = lax.broadcasted_iota(jnp.int32, (B, B), 0)
    wide = lax.broadcasted_iota(jnp.int32, (B, B), 1)
    unit = (tall == wide).astype(jnp.float32)
    work[:, B:] = unit
    up1, inv1 = eliminate(work)
    low21 = mul(corner[B:, :B], inv1, 1, 1)
    inv[:B, :B] = inv1
    inv[:B, B:] = jnp.zeros((B, B), jnp.float32)
    lower[:B, :B] = up1.T
    lower[:B, B:] = jnp.zeros((B, B), jnp.float32)
    lower[B:, :B] = low21

    @pl.when(jnp.logical_not(top))
    def _():
        mine_copy(0, row=row).wait_recv()

    @pl.when(relay)
    def _():
        mine_copy(1, row=row + 1).start()

    @pl.when(owner)
    def _():
        for d in (2, 1, 3):
            z_copy(d).start()
        rows_ref[piece] = mine[...]

    work[:, :B] = corner[B:, B:] - mul(low21, low21, 1, 1)
    work[:, B:] = unit
    up2, inv2 = eliminate(work)
    inv[B:, B:] = inv2
    inv[B:, :B] = -mul(inv2, mul(lower[B:, :B], inv[:B, :B], 1, 0), 1, 0)
    lower[B:, B:] = up2.T

    @pl.when(holder)
    def _():
        @pl.when(jnp.logical_not(owner))
        def _():
            piece_arrival(piece).wait_recv()

        for d in (2, 1, 3):
            x_copy(d).start()

    right[...] = mul(inv[...], mine[...], 1, 0)

    @pl.when(jnp.logical_not(holder & (piece == 0)))
    def _():
        piece_arrival(0).wait_recv()

    left[0] = mul(inv[...], rows_ref[0], 1, 0)

    @pl.when(jnp.logical_not(holder & (piece == 1)))
    def _():
        piece_arrival(1).wait_recv()

    left[1] = mul(inv[...], rows_ref[1], 1, 0)

    @pl.loop(0, 6)
    def _(n):
        block = left[n // 3, :, pl.ds(pl.multiple_of(lax.rem(n, 3) * NPIV, NPIV), NPIV)]
        here = pl.ds(pl.multiple_of(n * NPIV, NPIV), NPIV)
        out[here, :] = front[here, :] - mul(block, right[...], 0, 0)

        @pl.when(col == 0)
        def _():
            out[here, 0:NPIV] = block.T

    @pl.when(top)
    def _():
        out[0:NPIV, :] = jnp.zeros((NPIV, out.shape[1]), jnp.float32)

    @pl.when(first)
    def _():
        out[0:NPIV, 0:NPIV] = lower[...]

    @pl.when(first)
    def _():
        for d in range(1, COLS):
            corner_copy(d, col=d).wait_send()

    @pl.when(top)
    def _():
        for d in (4, 2, 6, 1):
            corner_copy(15 + d, row=d).wait_send()
        for d in (4, 2, 6, 1):
            mine_copy(d, row=d).wait_send()

    @pl.when(relay)
    def _():
        corner_copy(16, row=row + 1).wait_send()
        mine_copy(1, row=row + 1).wait_send()

    @pl.when(owner)
    def _():
        for d in (2, 1, 3):
            z_copy(d).wait_send()

    @pl.when(holder)
    def _():
        for d in (2, 1, 3):
            x_copy(d).wait_send()


def shards(parent_front, child_blocks, child_map, child_order):
    table = routing_table(child_map, child_order)
    shape = jax.ShapeDtypeStruct(parent_front.shape, jnp.float32)
    vmem = pl.BlockSpec(memory_space=pltpu.VMEM)
    width = parent_front.shape[1]
    front = pl.pallas_call(
        extend_kernel,
        out_shape=shape,
        in_specs=[
            pl.BlockSpec(memory_space=pltpu.SMEM),
            vmem,
            pl.BlockSpec(memory_space=pl.ANY),
        ],
        out_specs=vmem,
        scratch_shapes=[
            pltpu.VMEM((8, 8 * B, B), jnp.float32),
            pltpu.SemaphoreType.DMA((8,)),
            pltpu.VMEM((PARTS, COLS, 8, SUB, B), jnp.float32),
            pltpu.VMEM((PARTS, 12, 2, SUB, width), jnp.float32),
        ]
        + [pltpu.VMEM((COLS, 8, SUB, B), jnp.float32)] * PARTS
        + [pltpu.VMEM((16, 2, SUB, width), jnp.float32)] * PARTS
        + [
            pltpu.SemaphoreType.DMA((PARTS, COLS)),
            pltpu.SemaphoreType.DMA((PARTS, COLS)),
            pltpu.SemaphoreType.DMA((PARTS, 12)),
            pltpu.SemaphoreType.DMA((PARTS, ROWS)),
            pltpu.SemaphoreType.DMA((PARTS, ROWS)),
            pltpu.SemaphoreType.DMA((PARTS, 4)),
        ],
        compiler_params=pltpu.CompilerParams(
            collective_id=0, has_side_effects=True, vmem_limit_bytes=VMEM_LIMIT
        ),
        name="extend_add",
    )(table, parent_front, child_blocks)
    return pl.pallas_call(
        factor_kernel,
        out_shape=shape,
        in_specs=[vmem],
        out_specs=vmem,
        scratch_shapes=[
            pltpu.VMEM((NPIV, NPIV), jnp.float32),
            pltpu.VMEM((NPIV, width), jnp.float32),
            pltpu.VMEM((2, NPIV, width), jnp.float32),
            pltpu.VMEM((B, 2 * B), jnp.float32),
            pltpu.VMEM((NPIV, NPIV), jnp.float32),
            pltpu.VMEM((NPIV, NPIV), jnp.float32),
            pltpu.VMEM((2, NPIV, width), jnp.float32),
            pltpu.VMEM((NPIV, width), jnp.float32),
            pltpu.SemaphoreType.DMA((24,)),
            pltpu.SemaphoreType.DMA,
            pltpu.SemaphoreType.DMA((8,)),
            pltpu.SemaphoreType.DMA,
            pltpu.SemaphoreType.DMA((6,)),
            pltpu.SemaphoreType.DMA((2,)),
        ],
        compiler_params=pltpu.CompilerParams(
            collective_id=1, has_side_effects=True, vmem_limit_bytes=VMEM_LIMIT
        ),
        name="factor",
    )(front)


def solution(mesh):
    placed = (P("row", "col"), P("row", "col"), P(), P())
    return jax.shard_map(
        shards, mesh=mesh, in_specs=placed, out_specs=P("row", "col"), check_vma=False
    )
```

time: 924 us -> 267 us (0.29)
  the two profiles are of different devices: /device:TPU:39 before, /device:TPU:111 now
where the time goes in v1:
time: 267 us; the launch traced here: 266 us
  Pallas kernels  256 us (96%)
  local copies, waits for them, and re-layouts  7.84 us (3%)
    pallas_call x1, Pallas kernels, shards(): pl.pallas_call(extend_kernel, out_shape=shape, in_specs=[pl.BlockSpec(mem...  150 us
    pallas_call x1, Pallas kernels, shards(): pl.pallas_call(factor_kernel, out_shape=shape, in_specs=[vmem], out_specs...  106 us

profile of v1, /device:TPU:111, one launch (start us, length us, event | category | flops | bytes accessed | tf_op | source)
XLA Modules:
  0.0 266.3 jit_solution(11246258617711453059)
XLA Ops:
  0.0 0.7 and_select_fusion
  0.7 0.8 reshape.116
  1.5 0.1 convert_reduce_fusion
  1.6 0.1 select_reduce_fusion
  1.7 0.1 reshape.117
  1.7 0.1 slice.7
  1.8 0.1 slice.6
  1.9 0.1 copy.6
  2.0 0.1 copy.7
  2.1 0.1 copy.8
  2.2 0.2 convert_reduce_fusion.1
  2.4 0.8 select_reduce_fusion.1
  3.2 0.1 reshape.115
  3.3 0.1 sub.43
  3.4 0.1 copy.9
  3.5 0.1 min.12
  3.7 1.3 concatenate.3.tab
  5.0 150.1 %extend_add.1.front = f32[1536,768]{1,0:T(8,128)} custom-call(s32[834]{0:T(1024)} %concatenate.3.tab, f32[1536,768]{1,0:T(8,128)} %parent.1, f32[1024,1024]{1,0:T(8,128)} %child.1), custom_call_target="tpu_custom_call" | custom-call | tf_op jit(solution)/shard_map/extend_add/pallas_call | solution.py:513
  155.1 106.4 %factor.1 = f32[1536,768]{1,0:T(8,128)} custom-call(f32[1536,768]{1,0:T(8,128)} %extend_add.1.front), custom_call_target="tpu_custom_call" | custom-call | tf_op jit(solution)/shard_map/factor/pallas_call | solution.py:543
  261.5 4.8 %copy.11 = f32[1536,768]{1,0:T(8,128)} copy(f32[1536,768]{1,0:T(8,128)} %factor.1) | data formatting | bytes 9437184
  (9 shorter events, 0.1 us)

commit v2 on v1

v2 whole, which is shorter than its diff:
```python
import functools

import jax
import jax.numpy as jnp
from jax import lax
from jax.experimental import pallas as pl
from jax.experimental.pallas import tpu as pltpu
from jax.sharding import PartitionSpec as P

B = 128
NPIV = 256
ROWS = 8
COLS = 16
PARTS = 8
SUB = B // PARTS
MESH = pl.DeviceIdType.MESH
HI = lax.Precision.HIGHEST
VMEM_LIMIT = 66 * 1000 * 1000

T_INV = 0
T_SEL = 192
T_COL = 384
T_ROW = 640
T_ORD = 832
T_LEN = 834


def routing_table(child_map, child_order):
    kids, tiles = child_map.shape
    tile = jnp.arange(tiles, dtype=jnp.int32)
    place = jnp.arange(96, dtype=jnp.int32)
    hit = child_map[:, None, :] == place[None, :, None]
    inverse = jnp.sum(jnp.where(hit, tile[None, None, :] + 1, 0), axis=2) - 1
    window = child_map // 12
    same = (
        ((tile[:, None] - tile[None, :]) % ROWS == 0)
        & (tile[None, :] < tile[:, None])
    )
    rank = jnp.sum(
        (same[None] & (window[:, :, None] == window[:, None, :])).astype(jnp.int32), axis=2
    )
    slot = tile[None, :] % ROWS + ROWS * rank
    select = jnp.sum(jnp.where(hit, slot[:, None, :], 0), axis=2)
    grouped = child_map.reshape(kids, 8, 8)
    dest = jnp.arange(COLS, dtype=jnp.int32)
    step = jnp.arange(8, dtype=jnp.int32)
    col_pick = jnp.sum(
        jnp.where(
            (grouped // 6)[:, :, :, None] == dest[None, None, None, :],
            step[None, :, None, None],
            0,
        ),
        axis=1,
    )
    edges = jnp.arange(9, dtype=jnp.int32) * 12
    count = jnp.sum((grouped[:, :, :, None] < edges).astype(jnp.int32), axis=1)
    low, mid = count[:, :, 0:8:2], count[:, :, 1:9:2]
    extra = jnp.where(mid - low == 2, low + 1, mid + 1)
    row_pick = jnp.minimum(jnp.stack([low, mid, extra], axis=-1), 7)
    return jnp.concatenate(
        [
            inverse.reshape(-1),
            select.reshape(-1),
            col_pick.reshape(-1),
            row_pick.reshape(-1),
            child_order.reshape(-1),
        ]
    ).astype(jnp.int32)


def enter(row, col):
    barrier = pltpu.get_barrier_semaphore()
    for d in range(1, COLS):
        pl.semaphore_signal(
            barrier,
            inc=1,
            device_id={"col": lax.rem(col + d, COLS)},
            device_id_type=MESH,
        )
    for d in range(1, ROWS):
        pl.semaphore_signal(
            barrier,
            inc=1,
            device_id={"row": lax.rem(row + d, ROWS)},
            device_id_type=MESH,
        )
    pl.semaphore_wait(barrier, COLS + ROWS - 2)


def mul(a, b, ca, cb):
    return lax.dot_general(
        a,
        b,
        (((ca,), (cb,)), ((), ())),
        precision=HI,
        preferred_element_type=jnp.float32,
    )


def eliminate(work, first, last):
    wide = lax.broadcasted_iota(jnp.int32, (B, B), 1)
    one = lax.broadcasted_iota(jnp.int32, (1, B), 1)
    down = lax.broadcasted_iota(jnp.int32, (B, 1), 0)

    def body(j, carry):
        pivot_row = work[pl.ds(j, 1), :]
        pivot = jnp.sum(jnp.where(one == j, pivot_row[:, :B], 0.0), axis=1, keepdims=True)
        column = jnp.sum(jnp.where(wide == j, work[:, :B], 0.0), axis=1, keepdims=True)
        factor = jnp.where(down > j, column * (1.0 / pivot), 0.0)
        work[...] = work[...] - factor * pivot_row
        return carry

    lax.fori_loop(first, last, body, 0)


def eliminated(work):
    wide = lax.broadcasted_iota(jnp.int32, (B, B), 1)
    tall = lax.broadcasted_iota(jnp.int32, (B, B), 0)
    upper = work[:, :B]
    diagonal = jnp.sum(jnp.where(wide == tall, upper, 0.0), axis=1, keepdims=True)
    scale = lax.rsqrt(diagonal)
    scale = scale * (1.5 - 0.5 * diagonal * scale * scale)
    upper_factor = jnp.where(wide >= tall, upper * scale, 0.0)
    inverse = jnp.where(wide <= tall, work[:, B:] * scale, 0.0)
    return upper_factor, inverse


def front_kernel(
    tab,
    parent,
    child,
    out,
    kid_cols,
    send_c,
    send_r,
    send_p,
    recv_p,
    late,
    corner,
    mine,
    rows_ref,
    work,
    lower,
    inv,
    left,
    right,
    load_sem,
    cs,
    cr,
    rs,
    dr,
    br,
    fs,
    ps,
    pr,
    s_a,
    s_u,
    s_p,
    r_p,
    misc,
    *rest,
):
    recv_c = rest[:PARTS]
    recv_r = rest[PARTS:]
    row = lax.axis_index("row")
    col = lax.axis_index("col")
    chip = row // 2
    core = lax.rem(row, 2)
    other = 1 - core
    mate = row + 1 - 2 * core
    kid = col // 8
    slot = lax.rem(col, 8)
    zed = col // 4
    ex = lax.rem(col, 4)
    piece = lax.rem(ex, 2)
    owner = col // 2 == row
    holder = ex // 2 == core
    top = row == 0
    first = top & (col == 0)
    relay = (core == 0) & (row > 0)
    loads = [
        pltpu.make_async_copy(
            child.at[:, k * B : (k + 1) * B], kid_cols.at[k], load_sem.at[k]
        )
        for k in range(8)
    ]
    loads.append(pltpu.make_async_copy(parent, out, load_sem.at[8]))
    for load in loads:
        load.start()
    enter(row, col)
    for load in loads:
        load.wait()

    def copy(src, dst, send, recv, **where):
        return pltpu.make_async_remote_copy(
            src_ref=src,
            dst_ref=dst,
            send_sem=send,
            recv_sem=recv,
            device_id=where,
            device_id_type=MESH,
        )

    def pick_col(dest):
        return tab[T_COL + (kid * 8 + slot) * COLS + dest]

    def take_col(g, dest):
        k = pick_col(dest)
        return [kid_cols[k, t * B + g * SUB : t * B + (g + 1) * SUB, :] for t in range(8)]

    def col_copy(g, d):
        dest = lax.rem(col + d, COLS)
        return copy(
            send_c.at[g, dest], recv_c[g].at[col], cs.at[g, d], cr.at[g, col], col=dest
        )

    def col_arrival(g, d):
        source = lax.rem(col + d, COLS)
        return copy(
            send_c.at[g, source], recv_c[g].at[source], cs.at[g, d], cr.at[g, source], col=source
        )

    def pack_cols(g):
        @pl.loop(1, COLS)
        def _(d):
            dest = lax.rem(col + d, COLS)
            for t, part in enumerate(take_col(g, dest)):
                send_c[g, dest, t] = part

        for t, part in enumerate(take_col(g, col)):
            recv_c[g][col, t] = part

    def send_cols(g):
        @pl.loop(1, COLS)
        def _(d):
            col_copy(g, d).start()

    def panel_copy(d):
        dest = lax.rem(col + d, COLS)
        return copy(send_p.at[dest], recv_p.at[col], ps.at[d], pr.at[col], col=dest)

    def panel_arrival(d):
        source = lax.rem(col + d, COLS)
        return copy(send_p.at[source], recv_p.at[source], ps.at[d], pr.at[source], col=source)

    def late_copy():
        return copy(late, late, misc.at[0], misc.at[1], row=0)

    def late_arrival():
        return copy(late, late, misc.at[0], misc.at[1], row=1)

    def corner_copy(index, **where):
        return copy(corner, corner, s_a.at[index], misc.at[2], **where)

    def mine_copy(index, **where):
        return copy(mine, mine, s_u.at[index], misc.at[3], **where)

    def z_copy(d):
        to = lax.rem(zed + d, 4) * 4 + ex
        return copy(mine, rows_ref.at[piece], s_p.at[d - 1], r_p.at[piece], col=to)

    def x_copy(d):
        to = zed * 4 + lax.rem(ex + d, 4)
        return copy(
            rows_ref.at[piece], rows_ref.at[piece], s_p.at[2 + d], r_p.at[piece], col=to
        )

    def piece_arrival(index):
        return copy(mine, rows_ref.at[index], s_p.at[0], r_p.at[index], col=col)

    pack_cols(0)
    send_cols(0)

    @pl.when(row < 2)
    def _():
        @pl.loop(1, COLS)
        def _(d):
            dest = lax.rem(col + d, COLS)
            send_p[dest] = kid_cols[pick_col(dest), 0:B, :]

        recv_p[col] = kid_cols[pick_col(col), 0:B, :]

        @pl.loop(1, COLS)
        def _(d):
            panel_copy(d).start()

    pack_cols(1)
    send_cols(1)
    for g in range(2, PARTS):
        pack_cols(g)

    def direct_copy(g, dy, side):
        chip_to = lax.rem(chip + dy, 4)
        return copy(
            send_r.at[g, chip_to * 3 + side],
            recv_r[g].at[row],
            rs.at[g, dy * 3 + side],
            dr.at[g, row],
            row=chip_to * 2 + side,
        )

    def mate_copy(g):
        return copy(
            send_r.at[g, chip * 3 + other], recv_r[g].at[row], rs.at[g, 0], dr.at[g, row], row=mate
        )

    def extra_copy(g, dy):
        chip_to = lax.rem(chip + dy, 4)
        return copy(
            send_r.at[g, chip_to * 3 + 2],
            recv_r[g].at[8 + row],
            rs.at[g, dy * 3 + 2],
            br.at[g, row],
            row=chip_to * 2 + core,
        )

    def row_arrival(g, source, base, sem):
        return copy(
            send_r.at[g, 0], recv_r[g].at[base + source], rs.at[g, 0], sem.at[g, source], row=source
        )

    def forward_copy(g, dy):
        source = lax.rem(chip + dy, 4) * 2 + core
        return copy(
            recv_r[g].at[8 + source],
            recv_r[g].at[8 + source],
            fs.at[g, dy],
            br.at[g, source],
            row=mate,
        )

    def spread_rows(g):
        @pl.loop(1, COLS)
        def _(d):
            col_arrival(g, d).wait_recv()

        sources = []
        for h in range(2):
            for b in range(6):
                j = jnp.maximum(tab[T_INV + h * 96 + col * 6 + b], 0)
                sources.append(h * 8 + lax.rem(j, 8))

        @pl.loop(0, 12)
        def _(q):
            for h in range(2):
                k = tab[T_ROW + (h * 8 + row) * 12 + q]
                for b in range(6):
                    send_r[g, q, h, :, b * B : (b + 1) * B] = recv_c[g][sources[h * 6 + b], k]

        recv_r[g][row] = send_r[g, chip * 3 + core]
        recv_r[g][8 + row] = send_r[g, chip * 3 + 2]
        for dy in (2, 1, 3):
            extra_copy(g, dy).start()
            direct_copy(g, dy, 0).start()
            direct_copy(g, dy, 1).start()
        mate_copy(g).start()
        forward_copy(g, 0).start()

    def forward(g):
        for dy in range(1, 4):
            row_arrival(g, lax.rem(chip + dy, 4) * 2 + core, 8, br).wait_recv()
            forward_copy(g, dy).start()

    lane = lax.broadcasted_iota(jnp.int32, (1, B), 1)

    def land(g):
        for d in range(1, ROWS):
            row_arrival(g, lax.rem(row + d, ROWS), 0, dr).wait_recv()
        for dy in range(4):
            row_arrival(g, lax.rem(chip + dy, 4) * 2 + other, 8, br).wait_recv()
        alive = []
        for h in range(2):
            for b in range(6):
                j = tab[T_INV + h * 96 + col * 6 + b]
                limit = jnp.where(j < 0, 0, tab[T_ORD + h] - j * B)
                if b < 2:
                    limit = jnp.where(col == 0, 0, limit)
                alive.append(lane < limit)
        down = lax.broadcasted_iota(jnp.int32, (SUB, 1), 0) + g * SUB

        @pl.loop(0, 12)
        def _(a):
            start = pl.multiple_of(a * B + g * SUB, SUB)
            picks, lives = [], []
            for h in range(2):
                place = h * 96 + row * 12 + a
                i = tab[T_INV + place]
                limit = jnp.where(i < 0, 0, tab[T_ORD + h] - i * B)
                limit = jnp.where(row * 12 + a < 2, 0, limit)
                picks.append(tab[T_SEL + place])
                lives.append(down < limit)
            for b in range(6):
                span = slice(b * B, (b + 1) * B)
                total = out[pl.ds(start, SUB), span]
                for h in range(2):
                    part = recv_r[g][picks[h], h, :, span]
                    total = total + jnp.where(lives[h] & alive[h * 6 + b], part, 0.0)
                out[pl.ds(start, SUB), span] = total

    def frame(place, who, b):
        total = jnp.zeros((B, B), jnp.float32)
        for h in range(2):
            j = tab[T_INV + h * 96 + col * 6 + b]
            source = h * 8 + lax.rem(jnp.maximum(j, 0), 8)
            limit = jnp.where(j < 0, 0, tab[T_ORD + h] - j * B)
            limit = jnp.where(tab[T_INV + h * 96 + place] == who, limit, 0)
            total = total + jnp.where(lane < limit, recv_p[source], 0.0)
        return total

    tall = lax.broadcasted_iota(jnp.int32, (B, B), 0)
    wide = lax.broadcasted_iota(jnp.int32, (B, B), 1)

    def gather_panel():
        @pl.when(row < 2)
        def _():
            @pl.loop(1, COLS)
            def _(d):
                panel_arrival(d).wait_recv()

        @pl.when(row == 1)
        def _():
            for b in range(6):
                late[:, b * B : (b + 1) * B] = frame(1, 1, b)
            late_copy().start()

        @pl.when(top)
        def _():
            for place in range(2):
                here = slice(place * B, (place + 1) * B)
                for b in range(6):
                    span = slice(b * B, (b + 1) * B)
                    mine[here, span] = out[here, span] + frame(place, 0, b)
            late_arrival().wait_recv()
            mine[B:, :] = mine[B:, :] + late[...]

        @pl.when(first)
        def _():
            corner[...] = mine[:, 0:NPIV]
            for d in (2, 8, 1, 3, 4, 12, 5, 6, 7, 9, 10, 11, 13, 14, 15):
                corner_copy(d, col=d).start()

    def spread_panel():
        @pl.when(top & jnp.logical_not(first))
        def _():
            corner_copy(0, col=col).wait_recv()

        @pl.when(top)
        def _():
            for d in (4, 2, 6, 1):
                corner_copy(15 + d, row=d).start()
            for d in (4, 2, 6, 1):
                mine_copy(d, row=d).start()

    def relay_corner():
        @pl.when(relay)
        def _():
            corner_copy(0, row=row).wait_recv()
            corner_copy(16, row=row + 1).start()

    def begin_factor():
        @pl.when(core == 1)
        def _():
            corner_copy(0, row=row).wait_recv()

        work[:, :B] = corner[:B, :B]
        work[:, B:] = (tall == wide).astype(jnp.float32)
        eliminate(work, 0, 64)

    def share_mine():
        @pl.when(owner)
        def _():
            for d in (2, 1, 3):
                z_copy(d).start()
            rows_ref[piece] = mine[...]

    def half_factor():
        @pl.when(relay)
        def _():
            mine_copy(0, row=row).wait_recv()
            mine_copy(1, row=row + 1).start()

        @pl.when(core == 0)
        def _():
            share_mine()

        eliminate(work, 64, B - 1)
        up, low_inv = eliminated(work)
        low21 = mul(corner[B:, :B], low_inv, 1, 1)
        inv[:B, :B] = low_inv
        inv[:B, B:] = jnp.zeros((B, B), jnp.float32)
        lower[:B, :B] = up.T
        lower[:B, B:] = jnp.zeros((B, B), jnp.float32)
        lower[B:, :B] = low21
        work[:, :B] = corner[B:, B:] - mul(low21, low21, 1, 1)
        work[:, B:] = (tall == wide).astype(jnp.float32)

    def late_factor():
        @pl.when(core == 1)
        def _():
            mine_copy(0, row=row).wait_recv()
            share_mine()

        eliminate(work, 0, 64)

    def end_factor():
        @pl.when(holder)
        def _():
            @pl.when(jnp.logical_not(owner))
            def _():
                piece_arrival(piece).wait_recv()

            for d in (2, 1, 3):
                x_copy(d).start()

        eliminate(work, 64, B - 1)
        up, low_inv = eliminated(work)
        inv[B:, B:] = low_inv
        inv[B:, :B] = -mul(low_inv, mul(lower[B:, :B], inv[:B, :B], 1, 0), 1, 0)
        lower[B:, B:] = up.T

    def solve_own():
        right[...] = mul(inv[...], mine[...], 1, 0)

    def solve_rows():
        for index in range(2):

            @pl.when(jnp.logical_not(holder & (piece == index)))
            def _():
                piece_arrival(index).wait_recv()

            left[index] = mul(inv[...], rows_ref[index], 1, 0)

    def update():
        @pl.loop(0, 6)
        def _(n):
            block = left[n // 3, :, pl.ds(pl.multiple_of(lax.rem(n, 3) * NPIV, NPIV), NPIV)]
            here = pl.ds(pl.multiple_of(n * NPIV, NPIV), NPIV)
            out[here, :] = out[here, :] - mul(block, right[...], 0, 0)

            @pl.when(col == 0)
            def _():
                out[here, 0:NPIV] = block.T

        @pl.when(top)
        def _():
            out[0:NPIV, :] = jnp.zeros((NPIV, out.shape[1]), jnp.float32)

        @pl.when(first)
        def _():
            out[0:NPIV, 0:NPIV] = lower[...]

    hooks = [
        gather_panel,
        spread_panel,
        relay_corner,
        begin_factor,
        half_factor,
        late_factor,
        end_factor,
        solve_own,
    ]
    for g in range(PARTS):
        if g + 2 < PARTS:
            send_cols(g + 2)
        spread_rows(g)
        if g >= 1:
            forward(g - 1)
        if g >= 2:
            land(g - 2)
        hooks[g]()
    solve_rows()
    forward(PARTS - 1)
    land(PARTS - 2)
    update()
    land(PARTS - 1)

    for g in range(PARTS):

        @pl.loop(1, COLS)
        def _(d):
            col_copy(g, d).wait_send()

        for dy in range(1, 4):
            direct_copy(g, dy, 0).wait_send()
            direct_copy(g, dy, 1).wait_send()
            extra_copy(g, dy).wait_send()
        mate_copy(g).wait_send()
        for dy in range(4):
            forward_copy(g, dy).wait_send()

    @pl.when(row < 2)
    def _():
        @pl.loop(1, COLS)
        def _(d):
            panel_copy(d).wait_send()

    @pl.when(row == 1)
    def _():
        late_copy().wait_send()

    @pl.when(first)
    def _():
        for d in range(1, COLS):
            corner_copy(d, col=d).wait_send()

    @pl.when(top)
    def _():
        for d in (4, 2, 6, 1):
            corner_copy(15 + d, row=d).wait_send()
            mine_copy(d, row=d).wait_send()

    @pl.when(relay)
    def _():
        corner_copy(16, row=row + 1).wait_send()
        mine_copy(1, row=row + 1).wait_send()

    @pl.when(owner)
    def _():
        for d in (2, 1, 3):
            z_copy(d).wait_send()

    @pl.when(holder)
    def _():
        for d in (2, 1, 3):
            x_copy(d).wait_send()


def shards(parent_front, child_blocks, child_map, child_order):
    table = routing_table(child_map, child_order)
    width = parent_front.shape[1]
    wild = pl.BlockSpec(memory_space=pl.ANY)

    def vmem(*shape):
        return pltpu.VMEM(shape, jnp.float32)

    dma = pltpu.SemaphoreType.DMA
    return pl.pallas_call(
        front_kernel,
        out_shape=jax.ShapeDtypeStruct(parent_front.shape, jnp.float32),
        in_specs=[pl.BlockSpec(memory_space=pltpu.SMEM), wild, wild],
        out_specs=pl.BlockSpec(memory_space=pltpu.VMEM),
        scratch_shapes=[
            vmem(8, 8 * B, B),
            vmem(PARTS, COLS, 8, SUB, B),
            vmem(PARTS, 12, 2, SUB, width),
            vmem(COLS, B, B),
            vmem(COLS, B, B),
            vmem(B, width),
            vmem(NPIV, NPIV),
            vmem(NPIV, width),
            vmem(2, NPIV, width),
            vmem(B, 2 * B),
            vmem(NPIV, NPIV),
            vmem(NPIV, NPIV),
            vmem(2, NPIV, width),
            vmem(NPIV, width),
            dma((9,)),
            dma((PARTS, COLS)),
            dma((PARTS, COLS)),
            dma((PARTS, 12)),
            dma((PARTS, ROWS)),
            dma((PARTS, ROWS)),
            dma((PARTS, 4)),
            dma((COLS,)),
            dma((COLS,)),
            dma((24,)),
            dma((8,)),
            dma((6,)),
            dma((2,)),
            dma((4,)),
        ]
        + [vmem(COLS, 8, SUB, B)] * PARTS
        + [vmem(16, 2, SUB, width)] * PARTS,
        compiler_params=pltpu.CompilerParams(
            collective_id=0, has_side_effects=True, vmem_limit_bytes=VMEM_LIMIT
        ),
        name="front",
    )(table, parent_front, child_blocks)


def solution(mesh):
    placed = (P("row", "col"), P("row", "col"), P(), P())
    return jax.shard_map(
        shards, mesh=mesh, in_specs=placed, out_specs=P("row", "col"), check_vma=False
    )
```

time: 267 us -> 224 us (0.84)
  the two profiles are of different devices: /device:TPU:111 before, /device:TPU:100 now
where the time goes in v2:
time: 224 us; the launch traced here: 223 us
  Pallas kernels  214 us (96%)
  local copies, waits for them, and re-layouts  7.84 us (4%)
    pallas_call x1, Pallas kernels, shards(): pl.pallas_call(front_kernel, out_shape=jax.ShapeDtypeStruct(parent_front....  214 us
    unnamed x1, local copies, waits for them, and re-layouts  4.83 us

profile of v2, /device:TPU:100, one launch (start us, length us, event | category | flops | bytes accessed | tf_op | source)
XLA Modules:
  0.0 223.4 jit_solution(12062560090185240209)
XLA Ops:
  0.0 0.7 and_select_fusion
  0.7 0.8 reshape.116
  1.5 0.1 convert_reduce_fusion
  1.6 0.1 select_reduce_fusion
  1.7 0.1 reshape.117
  1.7 0.1 slice.7
  1.8 0.1 slice.6
  1.9 0.1 copy.6
  2.0 0.1 copy.7
  2.1 0.1 copy.8
  2.2 0.2 convert_reduce_fusion.1
  2.4 0.8 select_reduce_fusion.1
  3.2 0.1 reshape.115
  3.3 0.1 sub.43
  3.4 0.1 copy.9
  3.5 0.1 min.12
  3.7 1.3 concatenate.3.tab
  5.0 213.5 %front.1 = f32[1536,768]{1,0:T(8,128)} custom-call(s32[834]{0:T(1024)} %concatenate.3.tab, f32[1536,768]{1,0:T(8,128)} %parent.1, f32[1024,1024]{1,0:T(8,128)} %child.1), custom_call_target="tpu_custom_call" | custom-call | tf_op jit(solution)/shard_map/front/pallas_call | solution.py:637
  218.5 4.8 %copy.11 = f32[1536,768]{1,0:T(8,128)} copy(f32[1536,768]{1,0:T(8,128)} %front.1) | data formatting | bytes 9437184
  (9 shorter events, 0.1 us)

commit v3 on v2

--- a/solution.py
+++ b/solution.py
@@ -12,6 +12,10 @@
 ROWS = 8
 COLS = 16
 PARTS = 8
+Z_EVEN = 4
+Z_ODD = 4
+X_EVEN = 6
+X_ODD = 6
 SUB = B // PARTS
 MESH = pl.DeviceIdType.MESH
 HI = lax.Precision.HIGHEST
@@ -249,8 +253,17 @@
     def late_arrival():
         return copy(late, late, misc.at[0], misc.at[1], row=1)
 
-    def corner_copy(index, **where):
-        return copy(corner, corner, s_a.at[index], misc.at[2], **where)
+    def corner_x(d):
+        return copy(mine.at[:, 0:NPIV], corner, s_a.at[d - 1], misc.at[2], col=d)
+
+    def corner_z(d):
+        return copy(corner, corner, s_a.at[2 + d], misc.at[2], col=4 * d + ex)
+
+    def corner_mate():
+        return copy(corner, corner, s_a.at[6], misc.at[2], row=row + 1)
+
+    def corner_arrival():
+        return copy(corner, corner, s_a.at[6], misc.at[2], row=row)
 
     def mine_copy(index, **where):
         return copy(mine, mine, s_u.at[index], misc.at[3], **where)
@@ -329,11 +342,12 @@
             row=mate,
         )
 
-    def spread_rows(g):
+    def await_cols(g):
         @pl.loop(1, COLS)
         def _(d):
             col_arrival(g, d).wait_recv()
 
+    def spread_rows(g):
         sources = []
         for h in range(2):
             for b in range(6):
@@ -433,57 +447,123 @@
             late_arrival().wait_recv()
             mine[B:, :] = mine[B:, :] + late[...]
 
-        @pl.when(first)
-        def _():
+        @pl.when(top)
+        def _():
+            for d in (2, 6, 1):
+                mine_copy(d, row=d).start()
+
+        share_corner_x(top)
+
+    def share_mine():
+        for d in (2, 1, 3):
+            z_copy(d).start()
+        rows_ref[piece] = mine[...]
+
+    def share_corner_x(who):
+        @pl.when(who & (col == 0))
+        def _():
+            for d in (2, 1, 3):
+                corner_x(d).start()
             corner[...] = mine[:, 0:NPIV]
-            for d in (2, 8, 1, 3, 4, 12, 5, 6, 7, 9, 10, 11, 13, 14, 15):
-                corner_copy(d, col=d).start()
-
-    def spread_panel():
-        @pl.when(top & jnp.logical_not(first))
-        def _():
-            corner_copy(0, col=col).wait_recv()
-
-        @pl.when(top)
-        def _():
-            for d in (4, 2, 6, 1):
-                corner_copy(15 + d, row=d).start()
-            for d in (4, 2, 6, 1):
-                mine_copy(d, row=d).start()
-
-    def relay_corner():
-        @pl.when(relay)
-        def _():
-            corner_copy(0, row=row).wait_recv()
-            corner_copy(16, row=row + 1).start()
-
-    def begin_factor():
+
+    def share_corner_z(who):
+        @pl.when(who & (col > 0) & (col < 4))
+        def _():
+            corner_arrival().wait_recv()
+
+        @pl.when(who & (col < 4))
+        def _():
+            for d in (2, 1, 3):
+                corner_z(d).start()
+
+    def share_corner_mate(who):
+        @pl.when(who & (col > 3))
+        def _():
+            corner_arrival().wait_recv()
+
+        @pl.when(who)
+        def _():
+            corner_mate().start()
+
+    def half_copy(n):
+        half = mine.at[n * B : (n + 1) * B]
+        return copy(half, half, s_u.at[3], misc.at[3 + n], row=4)
+
+    def take_mine(who):
+        @pl.when(who & (row != 4))
+        def _():
+            mine_copy(0, row=row).wait_recv()
+
+        @pl.when(who & (row == 2))
+        def _():
+            half_copy(0).start()
+
+        @pl.when(who & (row == 6))
+        def _():
+            half_copy(1).start()
+
+        @pl.when(who & (row == 4))
+        def _():
+            half_copy(0).wait_recv()
+            half_copy(1).wait_recv()
+
+        share_corner_x(who & (core == 0))
+
+        @pl.when(who & (core == 0))
+        def _():
+            mine_copy(4, row=row + 1).start()
+
+    def share_z(who):
+        @pl.when(who & owner)
+        def _():
+            share_mine()
+
+    def share_rows(who):
+        @pl.when(who & holder & jnp.logical_not(owner))
+        def _():
+            piece_arrival(piece).wait_recv()
+
+        @pl.when(who & holder)
+        def _():
+            for d in (2, 1, 3):
+                x_copy(d).start()
+
+    below = row > 1
+
+    def panel_step(g):
+        if g == 0:
+            gather_panel()
+        if g == 1:
+            take_mine(row == 1)
+        if g == 2:
+            share_corner_z(top)
+            take_mine(relay & (row != 4))
+        if g == 3:
+            take_mine(row == 4)
+            take_mine(below & (core == 1) & (row != 5))
+        if g == 4:
+            take_mine(row == 5)
+            share_corner_mate(top)
+            share_corner_z(relay)
+        if g == 5:
+            share_corner_mate(relay)
+        if g == Z_EVEN:
+            share_z(core == 0)
+        if g == Z_ODD:
+            share_z(core == 1)
+        if g == X_EVEN:
+            share_rows(core == 0)
+        if g == X_ODD:
+            share_rows(core == 1)
+
+    def first_block():
         @pl.when(core == 1)
         def _():
-            corner_copy(0, row=row).wait_recv()
+            corner_arrival().wait_recv()
 
         work[:, :B] = corner[:B, :B]
         work[:, B:] = (tall == wide).astype(jnp.float32)
-        eliminate(work, 0, 64)
-
-    def share_mine():
-        @pl.when(owner)
-        def _():
-            for d in (2, 1, 3):
-                z_copy(d).start()
-            rows_ref[piece] = mine[...]
-
-    def half_factor():
-        @pl.when(relay)
-        def _():
-            mine_copy(0, row=row).wait_recv()
-            mine_copy(1, row=row + 1).start()
-
-        @pl.when(core == 0)
-        def _():
-            share_mine()
-
-        eliminate(work, 64, B - 1)
+        eliminate(work, 0, B - 1)
         up, low_inv = eliminated(work)
         low21 = mul(corner[B:, :B], low_inv, 1, 1)
         inv[:B, :B] = low_inv
@@ -494,25 +574,8 @@
         work[:, :B] = corner[B:, B:] - mul(low21, low21, 1, 1)
         work[:, B:] = (tall == wide).astype(jnp.float32)
 
-    def late_factor():
-        @pl.when(core == 1)
-        def _():
-            mine_copy(0, row=row).wait_recv()
-            share_mine()
-
-        eliminate(work, 0, 64)
-
-    def end_factor():
-        @pl.when(holder)
-        def _():
-            @pl.when(jnp.logical_not(owner))
-            def _():
-                piece_arrival(piece).wait_recv()
-
-            for d in (2, 1, 3):
-                x_copy(d).start()
-
-        eliminate(work, 64, B - 1)
+    def second_block():
+        eliminate(work, 0, B - 1)
         up, low_inv = eliminated(work)
         inv[B:, B:] = low_inv
         inv[B:, :B] = -mul(low_inv, mul(lower[B:, :B], inv[:B, :B], 1, 0), 1, 0)
@@ -549,29 +612,31 @@
         def _():
             out[0:NPIV, 0:NPIV] = lower[...]
 
-    hooks = [
-        gather_panel,
-        spread_panel,
-        relay_corner,
-        begin_factor,
-        half_factor,
-        late_factor,
-        end_factor,
-        solve_own,
-    ]
     for g in range(PARTS):
+        await_cols(g)
+        spread_rows(g)
+        panel_step(g)
         if g + 2 < PARTS:
             send_cols(g + 2)
-        spread_rows(g)
-        if g >= 1:
-            forward(g - 1)
         if g >= 2:
-            land(g - 2)
-        hooks[g]()
+            forward(g - 2)
+        if g >= 3:
+            land(g - 3)
+        if g == 5:
+            first_block()
+        if g == 6:
+            second_block()
+        if g == 7:
+            solve_own()
+    panel_step(PARTS)
+    for g in range(PARTS - 2, PARTS - 1):
+        forward(g)
+    for g in range(PARTS - 3, PARTS - 2):
+        land(g)
     solve_rows()
+    update()
+    land(PARTS - 2)
     forward(PARTS - 1)
-    land(PARTS - 2)
-    update()
     land(PARTS - 1)
 
     for g in range(PARTS):
@@ -598,21 +663,36 @@
     def _():
         late_copy().wait_send()
 
-    @pl.when(first)
-    def _():
-        for d in range(1, COLS):
-            corner_copy(d, col=d).wait_send()
+    @pl.when((core == 0) & (col == 0))
+    def _():
+        for d in range(1, 4):
+            corner_x(d).wait_send()
+
+    @pl.when((core == 0) & (col < 4))
+    def _():
+        for d in range(1, 4):
+            corner_z(d).wait_send()
+
+    @pl.when(core == 0)
+    def _():
+        corner_mate().wait_send()
 
     @pl.when(top)
     def _():
-        for d in (4, 2, 6, 1):
-            corner_copy(15 + d, row=d).wait_send()
+        for d in (2, 6, 1):
             mine_copy(d, row=d).wait_send()
 
     @pl.when(relay)
     def _():
-        corner_copy(16, row=row + 1).wait_send()
-        mine_copy(1, row=row + 1).wait_send()
+        mine_copy(4, row=row + 1).wait_send()
+
+    @pl.when(row == 2)
+    def _():
+        half_copy(0).wait_send()
+
+    @pl.when(row == 6)
+    def _():
+        half_copy(1).wait_send()
 
     @pl.when(owner)
     def _():
@@ -663,11 +743,11 @@
             dma((PARTS, 4)),
             dma((COLS,)),
             dma((COLS,)),
-            dma((24,)),
+            dma((7,)),
             dma((8,)),
             dma((6,)),
             dma((2,)),
-            dma((4,)),
+            dma((5,)),
         ]
         + [vmem(COLS, 8, SUB, B)] * PARTS
         + [vmem(16, 2, SUB, width)] * PARTS,

time: 224 us -> 182 us (0.81)
  the two profiles are of different devices: /device:TPU:100 before, /device:TPU:39 now
where the time goes in v3:
time: 182 us; the launch traced here: 181 us
  Pallas kernels  171 us (94%)
  local copies, waits for them, and re-layouts  7.84 us (4%)
  other arithmetic  1.92 us (1%)
    pallas_call x1, Pallas kernels, shards(): pl.pallas_call(front_kernel, out_shape=jax.ShapeDtypeStruct(parent_front....  171 us
    unnamed x1, local copies, waits for them, and re-layouts  4.83 us

profile of v3, /device:TPU:39, one launch (start us, length us, event | category | flops | bytes accessed | tf_op | source)
XLA Modules:
  0.0 180.6 jit_solution(9792064045877591331)
XLA Ops:
  0.0 0.7 and_select_fusion
  0.7 0.8 reshape.116
  1.5 0.1 convert_reduce_fusion
  1.6 0.1 select_reduce_fusion
  1.7 0.1 reshape.117
  1.7 0.1 slice.7
  1.8 0.1 slice.6
  1.9 0.1 copy.6
  2.0 0.1 copy.7
  2.1 0.1 copy.8
  2.2 0.2 convert_reduce_fusion.1
  2.4 0.8 select_reduce_fusion.1
  3.2 0.1 reshape.115
  3.3 0.1 sub.43
  3.4 0.1 copy.9
  3.5 0.1 min.12
  3.7 1.3 concatenate.3.tab
  5.0 170.7 %front.1 = f32[1536,768]{1,0:T(8,128)} custom-call(s32[834]{0:T(1024)} %concatenate.3.tab, f32[1536,768]{1,0:T(8,128)} %parent.1, f32[1024,1024]{1,0:T(8,128)} %child.1), custom_call_target="tpu_custom_call" | custom-call | tf_op jit(solution)/shard_map/front/pallas_call | solution.py:717
  175.7 4.8 %copy.11 = f32[1536,768]{1,0:T(8,128)} copy(f32[1536,768]{1,0:T(8,128)} %front.1) | data formatting | bytes 9437184
  (9 shorter events, 0.1 us)

commit v4 on v3

--- a/solution.py
+++ b/solution.py
@@ -19,7 +19,7 @@
 SUB = B // PARTS
 MESH = pl.DeviceIdType.MESH
 HI = lax.Precision.HIGHEST
-VMEM_LIMIT = 66 * 1000 * 1000
+VMEM_LIMIT = 56 * 1000 * 1000
 
 T_INV = 0
 T_SEL = 192
@@ -212,17 +212,43 @@
         k = pick_col(dest)
         return [kid_cols[k, t * B + g * SUB : t * B + (g + 1) * SUB, :] for t in range(8)]
 
-    def col_copy(g, d):
+    def col_copy(g, d, start):
         dest = lax.rem(col + d, COLS)
         return copy(
-            send_c.at[g, dest], recv_c[g].at[col], cs.at[g, d], cr.at[g, col], col=dest
-        )
-
-    def col_arrival(g, d):
+            send_c.at[g, dest, start:8],
+            recv_c[g].at[col, start:8],
+            cs.at[g, d],
+            cr.at[g, col],
+            col=dest,
+        )
+
+    def col_arrival(g, d, start):
         source = lax.rem(col + d, COLS)
         return copy(
-            send_c.at[g, source], recv_c[g].at[source], cs.at[g, d], cr.at[g, source], col=source
-        )
+            send_c.at[g, source, start:8],
+            recv_c[g].at[source, start:8],
+            cs.at[g, d],
+            cr.at[g, source],
+            col=source,
+        )
+
+    def each_col(g, action):
+        def run(start):
+            @pl.loop(1, COLS)
+            def _(d):
+                action(d, start)
+
+        if g == 0:
+            run(0)
+        else:
+
+            @pl.when(row < 2)
+            def _():
+                run(1)
+
+            @pl.when(row > 1)
+            def _():
+                run(0)
 
     def pack_cols(g):
         @pl.loop(1, COLS)
@@ -235,9 +261,7 @@
             recv_c[g][col, t] = part
 
     def send_cols(g):
-        @pl.loop(1, COLS)
-        def _(d):
-            col_copy(g, d).start()
+        each_col(g, lambda d, start: col_copy(g, d, start).start())
 
     def panel_copy(d):
         dest = lax.rem(col + d, COLS)
@@ -343,9 +367,7 @@
         )
 
     def await_cols(g):
-        @pl.loop(1, COLS)
-        def _(d):
-            col_arrival(g, d).wait_recv()
+        each_col(g, lambda d, start: col_arrival(g, d, start).wait_recv())
 
     def spread_rows(g):
         sources = []
@@ -430,6 +452,11 @@
             @pl.loop(1, COLS)
             def _(d):
                 panel_arrival(d).wait_recv()
+
+            @pl.loop(0, COLS)
+            def _(source):
+                for g in range(1, PARTS):
+                    recv_c[g][source, 0] = recv_p[source, g * SUB : (g + 1) * SUB, :]
 
         @pl.when(row == 1)
         def _():
@@ -615,9 +642,9 @@
     for g in range(PARTS):
         await_cols(g)
         spread_rows(g)
-        panel_step(g)
         if g + 2 < PARTS:
             send_cols(g + 2)
+        panel_step(g)
         if g >= 2:
             forward(g - 2)
         if g >= 3:
@@ -641,9 +668,7 @@
 
     for g in range(PARTS):
 
-        @pl.loop(1, COLS)
-        def _(d):
-            col_copy(g, d).wait_send()
+        each_col(g, lambda d, start: col_copy(g, d, start).wait_send())
 
         for dy in range(1, 4):
             direct_copy(g, dy, 0).wait_send()
@@ -716,7 +741,7 @@
     dma = pltpu.SemaphoreType.DMA
     return pl.pallas_call(
         front_kernel,
-        out_shape=jax.ShapeDtypeStruct(parent_front.shape, jnp.float32),
+        out_shape=pltpu.VMEM(parent_front.shape, jnp.float32),
         in_specs=[pl.BlockSpec(memory_space=pltpu.SMEM), wild, wild],
         out_specs=pl.BlockSpec(memory_space=pltpu.VMEM),
         scratch_shapes=[

time: 182 us -> 168 us (0.923)
  Pallas kernels: 171 us -> 161 us
  local copies, waits for them, and re-layouts: 7.84 us -> 5.2 us
    pallas_call x1, Pallas kernels: 171 us -> 161 us  [shards(): pl.pallas_call(front_kernel, out_shape=pltpu.VMEM(parent_front.shape, jnp...]
    unnamed x1, local copies, waits for them, and re-layouts: 4.83 us -> 2.19 us
where the time goes in v4:
time: 168 us
  Pallas kernels  161 us (96%)
  local copies, waits for them, and re-layouts  5.2 us (3%)
  other arithmetic  1.92 us (1%)
    pallas_call x1, Pallas kernels, shards(): pl.pallas_call(front_kernel, out_shape=pltpu.VMEM(parent_front.shape, jnp...  161 us

profile of v4, /device:TPU:39, one launch (start us, length us, event | category | flops | bytes accessed | tf_op | source)
XLA Modules:
  0.0 167.7 jit_solution(15008753726451939875)
XLA Ops:
  0.0 0.7 and_select_fusion
  0.7 0.8 reshape.116
  1.5 0.1 convert_reduce_fusion
  1.6 0.1 select_reduce_fusion
  1.7 0.1 reshape.117
  1.7 0.1 slice.7
  1.8 0.1 slice.6
  1.9 0.1 copy.6
  2.0 0.1 copy.7
  2.1 0.1 copy.8
  2.2 0.2 convert_reduce_fusion.1
  2.4 0.8 select_reduce_fusion.1
  3.2 0.1 reshape.115
  3.3 0.1 sub.43
  3.4 0.1 copy.9
  3.5 0.1 min.12
  3.7 1.3 concatenate.3.tab
  5.0 160.5 %front.1 = f32[1536,768]{1,0:T(8,128)S(1)} custom-call(s32[834]{0:T(1024)} %concatenate.3.tab, f32[1536,768]{1,0:T(8,128)} %parent.1, f32[1024,1024]{1,0:T(8,128)} %child.1), custom_call_target="tpu_custom_call" | custom-call | tf_op jit(solution)/shard_map/front/pallas_call | solution.py:742
  165.5 2.2 %copy.11 = f32[1536,768]{1,0:T(8,128)} copy(f32[1536,768]{1,0:T(8,128)S(1)} %front.1) | data formatting | bytes 9437184
  (9 shorter events, 0.1 us)

commit v5 on v4

--- a/solution.py
+++ b/solution.py
@@ -645,10 +645,10 @@
         if g + 2 < PARTS:
             send_cols(g + 2)
         panel_step(g)
-        if g >= 2:
-            forward(g - 2)
         if g >= 3:
-            land(g - 3)
+            forward(g - 3)
+        if g >= 4:
+            land(g - 4)
         if g == 5:
             first_block()
         if g == 6:
@@ -656,9 +656,9 @@
         if g == 7:
             solve_own()
     panel_step(PARTS)
-    for g in range(PARTS - 2, PARTS - 1):
+    for g in range(PARTS - 3, PARTS - 1):
         forward(g)
-    for g in range(PARTS - 3, PARTS - 2):
+    for g in range(PARTS - 4, PARTS - 2):
         land(g)
     solve_rows()
     update()

time: 168 us -> 168 us (level)
  no operation moved by 1% of the time
where the time goes in v5:
time: 168 us; the launch traced here: 167 us
  Pallas kernels  160 us (95%)
  local copies, waits for them, and re-layouts  5.2 us (3%)
  other arithmetic  1.92 us (1%)
    pallas_call x1, Pallas kernels, shards(): pl.pallas_call(front_kernel, out_shape=pltpu.VMEM(parent_front.shape, jnp...  160 us

profile of v5, /device:TPU:39, one launch (start us, length us, event | category | flops | bytes accessed | tf_op | source)
XLA Modules:
  0.0 167.5 jit_solution(7646680451214386292)
XLA Ops:
  0.0 0.7 and_select_fusion
  0.7 0.8 reshape.116
  1.5 0.1 convert_reduce_fusion
  1.6 0.1 select_reduce_fusion
  1.7 0.1 reshape.117
  1.7 0.1 slice.7
  1.8 0.1 slice.6
  1.9 0.1 copy.6
  2.0 0.1 copy.7
  2.1 0.1 copy.8
  2.2 0.2 convert_reduce_fusion.1
  2.4 0.8 select_reduce_fusion.1
  3.2 0.1 reshape.115
  3.3 0.1 sub.43
  3.4 0.1 copy.9
  3.5 0.1 min.12
  3.7 1.3 concatenate.3.tab
  5.0 160.3 %front.1 = f32[1536,768]{1,0:T(8,128)S(1)} custom-call(s32[834]{0:T(1024)} %concatenate.3.tab, f32[1536,768]{1,0:T(8,128)} %parent.1, f32[1024,1024]{1,0:T(8,128)} %child.1), custom_call_target="tpu_custom_call" | custom-call | tf_op jit(solution)/shard_map/front/pallas_call | solution.py:742
  165.3 2.2 %copy.11 = f32[1536,768]{1,0:T(8,128)} copy(f32[1536,768]{1,0:T(8,128)S(1)} %front.1) | data formatting | bytes 9437184
  (9 shorter events, 0.1 us)
